TPU v7x, 32 devices: a whole 2x2x4 slice. The times are simulated.
32 devices in a mesh: seq: 8 (over z, x), head: 4 (over y, core).
Axes of the slice: x: 2, y: 2, z: 4, core: 2. Of those that a mesh axis runs over, the one named last changes fastest.
Arguments:
- query: bfloat16 [4096, 4096], P(('seq', 'head')), may hold values from -6 to 6
- key: bfloat16 [4096, 1024], P(('seq', 'head')), may hold values from -6 to 6
- value: bfloat16 [4096, 1024], P(('seq', 'head')), may hold values from -6 to 6
- out: bfloat16 [4096, 4096], P(('seq', 'head')), may hold values from -4 to 4
- output_gradient: bfloat16 [4096, 4096], P(('seq', 'head')), may hold values from -6 to 6
- log_sum_exp: float32 [4096, 32], P(('seq', 'head')), may hold values from 4 to 7
- segment_ids: int32 [4096], replicated, may hold values from 0 to 3, never falling along the last dimension, each value on 1 to 1536 neighbouring positions
Outputs:
- d_query: bfloat16 [4096, 4096], P(('seq', 'head'))
- key_gradient: bfloat16 [4096, 1024], P(('seq', 'head'))
- value_gradient: bfloat16 [4096, 1024], P(('seq', 'head'))
Inputs may be any that keep to these rules, and one draw needn't show every extreme that they name: `segment_ids`: never falls along the positions; a document holds at most 1536 positions, and one holds exactly 1536.
All inputs are finite; a program needn't handle non-finite values.
Results may differ from a plain program's by a relative error of at most 0.0071.
Values may be sent and summed in bfloat16 or wider, within the bound.
A program may use at most 128 MiB of HBM per device.

v0:
```python
import functools
import math

import jax
import jax.numpy as jnp
from jax import lax
from jax.experimental import pallas as pl
from jax.experimental.pallas import tpu as pltpu
from jax.sharding import PartitionSpec as P

HEAD_SIZE = 128
REACH = 3
TILE = 256
LOG2E = math.log2(math.e)
MESH = pl.DeviceIdType.MESH
NT = (((1,), (1,)), ((), ()))


def dot(a, b):
    return jnp.dot(a, b, preferred_element_type=jnp.float32)


def dot_nt(a, b):
    return lax.dot_general(a, b, NT, preferred_element_type=jnp.float32)


def kernel(
    n, seqs, groups, width,
    q_ref, e_ref, k_ref, v_ref, st_ref, start_ref,
    dq_out, dk_out, dv_out,
    qb, eb, stb, kw, vw, dqt, acck, accv, ownk, ownv, part_s, part_r, dqs, dks, dvs,
    loc_sem, in_s, in_r, fw_s, fw_r, pt_s, pt_r, out_s, out_r,
):
    s = lax.axis_index("seq")
    h = lax.axis_index("head")
    rows = q_ref.shape[0]
    block = rows * n
    cols = q_ref.shape[1] // n
    kcols = k_ref.shape[1] // n
    hd = HEAD_SIZE
    gw = width * hd
    halves = block // TILE
    scale = 1.0 / math.sqrt(hd)
    heads = groups * width

    def at(index, size):
        return pl.ds(pl.multiple_of(index * size, size), size)

    barrier = pltpu.get_barrier_semaphore()
    for r in range(1, n):
        pl.semaphore_signal(barrier, inc=1, device_id={"head": lax.rem(h + r, n)}, device_id_type=MESH)
    for d in range(1, REACH + 1):
        @pl.when(s + d < seqs)
        def _():
            pl.semaphore_signal(barrier, inc=1, device_id={"seq": s + d}, device_id_type=MESH)

        @pl.when(s >= d)
        def _():
            pl.semaphore_signal(barrier, inc=1, device_id={"seq": s - d}, device_id_type=MESH)
    pl.semaphore_wait(barrier, n - 1 + jnp.minimum(s, REACH) + jnp.minimum(seqs - 1 - s, REACH))

    def entry(kind, owner, me):
        if kind == 0:
            return st_ref.at[owner], stb.at[:, at(me, rows)]
        if kind == 1:
            return k_ref.at[:, at(owner, kcols)], kw.at[0, at(me, rows), :]
        if kind == 2:
            return v_ref.at[:, at(owner, kcols)], vw.at[0, at(me, rows), :]
        g, which = (kind - 3) // 2, (kind - 3) % 2
        src, dst = ((q_ref, qb), (e_ref, eb))[which]
        from_cols = pl.ds(pl.multiple_of(owner * cols + g * gw, hd), gw)
        return src.at[:, from_cols], dst.at[at(me, rows), pl.ds(g * gw, gw)]

    kinds = 3 + 2 * groups

    def entry_copy(kind, r):
        peer = lax.rem(h + r, n)
        src, dst = entry(kind, peer, h)
        return pltpu.make_async_remote_copy(
            src_ref=src, dst_ref=dst, send_sem=in_s.at[kind, r - 1], recv_sem=in_r.at[kind, r - 1],
            device_id={"head": peer}, device_id_type=MESH)

    def entry_own(kind):
        src, dst = entry(kind, h, h)
        return pltpu.make_async_copy(src, dst, loc_sem.at[kind])

    for kind in (1, 2, 0) + tuple(range(3, kinds)):
        entry_own(kind).start()
        for r in range(1, n):
            entry_copy(kind, r).start()

    def entry_wait(kind):
        entry_own(kind).wait()
        for r in range(1, n):
            entry_copy(kind, r).wait_recv()

    def forward(which, d):
        buf = (kw, vw)[which]
        return pltpu.make_async_remote_copy(
            src_ref=buf.at[0], dst_ref=buf.at[d], send_sem=fw_s.at[which, d - 1], recv_sem=fw_r.at[which, d - 1],
            device_id={"seq": s + d}, device_id_type=MESH)

    def partial(which, g, d):
        return pltpu.make_async_remote_copy(
            src_ref=part_s.at[which, g, d - 1], dst_ref=part_r.at[which, g, d - 1],
            send_sem=pt_s.at[which, g, d - 1], recv_sem=pt_r.at[which, g, d - 1],
            device_id={"seq": s - d}, device_id_type=MESH)

    def leave(which, g, owner):
        src, dst, size, full = ((dqs, dq_out, gw, cols), (dks, dk_out, hd, kcols), (dvs, dv_out, hd, kcols))[which]
        to_cols = pl.ds(pl.multiple_of(h * full + g * size, hd), size)
        return src.at[at(owner, rows), pl.ds(g * size, size)], dst.at[:, to_cols]

    def leave_copy(which, g, r):
        peer = lax.rem(h + r, n)
        src, dst = leave(which, g, peer)
        return pltpu.make_async_remote_copy(
            src_ref=src, dst_ref=dst, send_sem=out_s.at[which, g, r - 1], recv_sem=out_r.at[which, g, r - 1],
            device_id={"head": peer}, device_id_type=MESH)

    def leave_own(which, g):
        src, dst = leave(which, g, h)
        return pltpu.make_async_copy(src, dst, loc_sem.at[kinds + which * groups + g])

    def leave_start(which, g):
        for r in range(1, n):
            leave_copy(which, g, r).start()
        leave_own(which, g).start()

    for kind in (1, 2):
        entry_wait(kind)
    for d in range(1, REACH + 1):
        @pl.when(s + d < seqs)
        def _():
            forward(0, d).start()
            forward(1, d).start()
    entry_wait(0)

    row_at = lax.broadcasted_iota(jnp.int32, (TILE, TILE), 0)
    col_at = lax.broadcasted_iota(jnp.int32, (TILE, TILE), 1)

    def tile(g, d, hf, qt):
        k_rows, q_rows = at(hf, TILE), at(qt, TILE)
        kcol = pl.ds(g * hd, hd)
        key, val = kw[d, k_rows, kcol], vw[d, k_rows, kcol]
        key_t = key.T
        first = start_ref[0:1, q_rows] - (hf * TILE - d * block)
        allowed = row_at >= first
        if d == 0:
            allowed &= row_at + (hf - qt) * TILE <= col_at
        add_k = add_v = None
        for m in range(width):
            hcol = pl.ds((g * width + m) * hd, hd)
            query, grad = qb[q_rows, hcol], eb[q_rows, hcol]
            lse = stb[g * width + m : g * width + m + 1, q_rows]
            delta = stb[heads + g * width + m : heads + g * width + m + 1, q_rows]
            scores = dot_nt(key, query)
            probs = jnp.exp2(jnp.where(allowed, scores * (scale * LOG2E) - lse, -jnp.inf))
            dprobs = dot_nt(val, grad)
            dscores = (probs * (dprobs - delta)).astype(jnp.bfloat16)
            one_v = dot(probs.astype(jnp.bfloat16), grad)
            one_k = dot(dscores, query)
            add_v = one_v if m == 0 else add_v + one_v
            add_k = one_k if m == 0 else add_k + one_k
            dqt[m, :, q_rows] += dot(key_t, dscores)
        acck[k_rows, :] += add_k
        accv[k_rows, :] += add_v

    def compute(g, d):
        acck[...] = jnp.zeros_like(acck)
        accv[...] = jnp.zeros_like(accv)

        @pl.loop(0, halves)
        def _(hf):
            low = hf if d == 0 else 0
            high = hf + 1 if d == REACH else halves

            @pl.loop(low, high)
            def _(qt):
                tile(g, d, hf, qt)

    def finish(g):
        for d in range(1, REACH + 1):
            @pl.when(s + d < seqs)
            def _():
                partial(0, g, d).wait_recv()
                partial(1, g, d).wait_recv()
                ownk[g] += part_r[0, g, d - 1].astype(jnp.float32)
                ownv[g] += part_r[1, g, d - 1].astype(jnp.float32)
        dks[:, g * hd : (g + 1) * hd] = (ownk[g] * scale).astype(jnp.bfloat16)
        dvs[:, g * hd : (g + 1) * hd] = ownv[g].astype(jnp.bfloat16)
        leave_start(1, g)
        leave_start(2, g)

    for g in range(groups):
        entry_wait(3 + 2 * g)
        entry_wait(4 + 2 * g)
        dqt[...] = jnp.zeros_like(dqt)
        order = range(REACH + 1) if g == 0 else range(REACH, -1, -1)
        for step, d in enumerate(order):
            if d == 0:
                compute(g, 0)
                ownk[g] = acck[...]
                ownv[g] = accv[...]
            else:
                @pl.when(s >= d)
                def _():
                    if g == 0:
                        forward(0, d).wait_recv()
                        forward(1, d).wait_recv()
                    compute(g, d)
                    part_s[0, g, d - 1] = acck[...].astype(jnp.bfloat16)
                    part_s[1, g, d - 1] = accv[...].astype(jnp.bfloat16)
                    partial(0, g, d).start()
                    partial(1, g, d).start()
            if g > 0 and step == 1:
                finish(g - 1)
        for m in range(width):
            here = (g * width + m) * hd
            dqs[:, here : here + hd] = (dqt[m] * scale).T.astype(jnp.bfloat16)
        leave_start(0, g)
    finish(groups - 1)

    for which in range(3):
        for g in range(groups):
            leave_own(which, g).wait()
            for r in range(1, n):
                leave_copy(which, g, r).wait()
    for kind in range(kinds):
        for r in range(1, n):
            entry_copy(kind, r).wait_send()
    for d in range(1, REACH + 1):
        @pl.when(s + d < seqs)
        def _():
            forward(0, d).wait_send()
            forward(1, d).wait_send()

        @pl.when(s >= d)
        def _():
            for g in range(groups):
                partial(0, g, d).wait_send()
                partial(1, g, d).wait_send()


def shards(query, key, value, out, output_gradient, log_sum_exp, segment_ids):
    n, seqs = lax.axis_size("head"), lax.axis_size("seq")
    hd = HEAD_SIZE
    rows = query.shape[0]
    block = rows * n
    cols, kcols = query.shape[1] // n, key.shape[1] // n
    groups, width = kcols // hd, cols // kcols
    heads = groups * width
    delta = jnp.sum(
        (output_gradient.astype(jnp.float32) * out.astype(jnp.float32)).reshape(rows, -1, hd), axis=2
    )
    stats = jnp.concatenate(
        [(log_sum_exp * LOG2E).T.reshape(n, heads, rows), delta.T.reshape(n, heads, rows)], axis=1
    )
    base = lax.axis_index("seq") * block
    mine = lax.dynamic_slice_in_dim(segment_ids, base, block, 0)
    start = jnp.sum((segment_ids[:, None] < mine[None, :]).astype(jnp.int32), axis=0)[None, :] - base
    bf16, f32 = jnp.bfloat16, jnp.float32
    kinds = 3 + 2 * groups
    vmem = pl.BlockSpec(memory_space=pltpu.VMEM)
    dma = pltpu.SemaphoreType.DMA
    return pl.pallas_call(
        functools.partial(kernel, n, seqs, groups, width),
        out_shape=[
            jax.ShapeDtypeStruct(query.shape, bf16),
            jax.ShapeDtypeStruct(key.shape, bf16),
            jax.ShapeDtypeStruct(value.shape, bf16),
        ],
        in_specs=[vmem] * 6,
        out_specs=[vmem] * 3,
        scratch_shapes=[
            pltpu.VMEM((block, cols), bf16),
            pltpu.VMEM((block, cols), bf16),
            pltpu.VMEM((2 * heads, block), f32),
            pltpu.VMEM((REACH + 1, block, kcols), bf16),
            pltpu.VMEM((REACH + 1, block, kcols), bf16),
            pltpu.VMEM((width, hd, block), f32),
            pltpu.VMEM((block, hd), f32),
            pltpu.VMEM((block, hd), f32),
            pltpu.VMEM((groups, block, hd), f32),
            pltpu.VMEM((groups, block, hd), f32),
            pltpu.VMEM((2, groups, REACH, block, hd), bf16),
            pltpu.VMEM((2, groups, REACH, block, hd), bf16),
            pltpu.VMEM((block, cols), bf16),
            pltpu.VMEM((block, kcols), bf16),
            pltpu.VMEM((block, kcols), bf16),
            dma((kinds + 3 * groups,)),
            dma((kinds, n - 1)),
            dma((kinds, n - 1)),
            dma((2, REACH)),
            dma((2, REACH)),
            dma((2, groups, REACH)),
            dma((2, groups, REACH)),
            dma((3, groups, n - 1)),
            dma((3, groups, n - 1)),
        ],
        compiler_params=pltpu.CompilerParams(collective_id=0, has_side_effects=True),
    )(query, output_gradient, key, value, stats, start)


def solution(mesh):
    placed = (P(("seq", "head"), None),) * 6 + (P(),)
    return jax.shard_map(
        lambda *a: tuple(shards(*a)),
        mesh=mesh,
        in_specs=placed,
        out_specs=(P(("seq", "head"), None),) * 3,
        check_vma=False,
    )
```

profile of v0, /device:TPU:15, one launch (start us, length us, event | category | flops | bytes accessed | tf_op | source)
XLA Modules:
  0.0 104.1 jit_solution(10660679707290989533)
XLA Ops:
  0.6 1.8 %multiply_bitcast_fusion = f32[16,8,32,128]{3,1,2,0:T(8,128)S(1)} fusion(bf16[128,4096]{1,0:T(8,128)(2,1)} %param.10, bf16[128,4096]{1,0:T(8,128)(2,1)} %e_ref.1), kind=kLoop, calls=%fused_computation.1 | loop fusion | flops 1572864 | bytes 4194304
  2.4 0.4 copy.12
  2.8 0.0 copy-start.2
  2.8 0.0 copy-start.3
  2.8 0.6 reduce_sum.18
  3.4 0.1 copy.11
  3.5 0.0 copy-done.2
  3.5 0.6 pad_maximum_fusion.st_ref
  4.2 0.0 copy-done.3
  4.2 0.1 dynamic_slice.3
  4.2 1.0 convert_reduce_fusion
  5.2 0.6 broadcast_subtract_fusion
  5.8 94.6 %shard_map.94 = (bf16[128,4096]{1,0:T(8,128)(2,1)}, bf16[128,1024]{1,0:T(8,128)(2,1)}, bf16[128,1024]{1,0:T(8,128)(2,1)}) custom-call(bf16[128,4096]{1,0:T(8,128)(2,1)} %q_ref.1, bf16[128,4096]{1,0:T(8,128)(2,1)} %e_ref.1, bf16[128,1024]{1,0:T(8,128)(2,1)} %k_ref.1, bf16[128,1024]{1,0:T(8,128)(2,1)} %v_ref.1, f32[4,16,128]{2,1,0:T(8,128)} %pad_maximum_fusion.st_ref, ...), custom_call_target="tpu_custom_call" | custom-call | tf_op jit(solution)/shard_map/pallas_call | solution.py:266
  100.4 0.0 copy-start.1
  100.4 0.0 copy-start
  100.4 2.3 %copy.16 = bf16[128,4096]{1,0:T(8,128)(2,1)} copy(bf16[128,4096]{1,0:T(8,128)(2,1)} %get-tuple-element.6) | data formatting | bytes 2097152
  102.7 0.0 copy-done.1
  102.7 0.7 copy.17
  103.4 0.0 copy-done
  103.4 0.7 copy.18
  (1 shorter events, 0.0 us)
Async XLA Ops:
  2.8 0.7 copy-start.2
  2.8 1.3 %copy-start.3 = (s32[4096]{0:T(1024)S(1)}, s32[4096]{0:T(1024)}, u32[]{:S(2)}) copy-start(s32[4096]{0:T(1024)} %param.13) | copy-start | bytes 49156
  100.4 2.4 %copy-start.1 = (bf16[128,1024]{1,0:T(8,128)(2,1)S(1)}, bf16[128,1024]{1,0:T(8,128)(2,1)}, u32[]{:S(2)}) copy-start(bf16[128,1024]{1,0:T(8,128)(2,1)} %get-tuple-element.7) | copy-start | bytes 786436
  100.4 3.1 %copy-start = (bf16[128,1024]{1,0:T(8,128)(2,1)S(1)}, bf16[128,1024]{1,0:T(8,128)(2,1)}, u32[]{:S(2)}) copy-start(bf16[128,1024]{1,0:T(8,128)(2,1)} %get-tuple-element.8) | copy-start | bytes 786436
where the time goes:
time: 104 us
  Pallas kernels  94.6 us (91%)
  other arithmetic  4.59 us (4%)
  local copies, waits for them, and re-layouts  4.29 us (4%)
    pallas_call x1, Pallas kernels, shards(): pl.pallas_call(functools.partial(kernel, n, seqs, groups, width), out_sha...  94.6 us
    unnamed x12, local copies, waits for them, and re-layouts  4.16 us

commit v1 on v0

--- a/solution.py
+++ b/solution.py
@@ -28,7 +28,7 @@
     n, seqs, groups, width,
     q_ref, e_ref, k_ref, v_ref, st_ref, start_ref,
     dq_out, dk_out, dv_out,
-    qb, eb, stb, kw, vw, dqt, acck, accv, ownk, ownv, part_s, part_r, dqs, dks, dvs,
+    qb, eb, stb, kv, dqt, acck, accv, ownk, ownv, part_s, part_r, dqs, dks, dvs,
     loc_sem, in_s, in_r, fw_s, fw_r, pt_s, pt_r, out_s, out_r,
 ):
     s = lax.axis_index("seq")
@@ -44,34 +44,42 @@
     heads = groups * width
 
     def at(index, size):
-        return pl.ds(pl.multiple_of(index * size, size), size)
+        return pl.ds(index * size if isinstance(index, int) else pl.multiple_of(index * size, size), size)
+
+    side = s + 1 - 2 * lax.rem(s, 2)
+    even = lax.rem(s, 2) == 0
+    odd = lax.rem(s, 2) == 1
+    has_up, has_down = s + 2 < seqs, s >= 2
 
     barrier = pltpu.get_barrier_semaphore()
     for r in range(1, n):
         pl.semaphore_signal(barrier, inc=1, device_id={"head": lax.rem(h + r, n)}, device_id_type=MESH)
-    for d in range(1, REACH + 1):
-        @pl.when(s + d < seqs)
-        def _():
-            pl.semaphore_signal(barrier, inc=1, device_id={"seq": s + d}, device_id_type=MESH)
-
-        @pl.when(s >= d)
-        def _():
-            pl.semaphore_signal(barrier, inc=1, device_id={"seq": s - d}, device_id_type=MESH)
-    pl.semaphore_wait(barrier, n - 1 + jnp.minimum(s, REACH) + jnp.minimum(seqs - 1 - s, REACH))
+    pl.semaphore_signal(barrier, inc=1, device_id={"seq": side}, device_id_type=MESH)
+
+    @pl.when(has_up)
+    def _():
+        pl.semaphore_signal(barrier, inc=1, device_id={"seq": s + 2}, device_id_type=MESH)
+
+    @pl.when(has_down)
+    def _():
+        pl.semaphore_signal(barrier, inc=1, device_id={"seq": s - 2}, device_id_type=MESH)
+
+    pl.semaphore_wait(barrier, n + jnp.minimum(s // 2, 1) + jnp.minimum((seqs - 1 - s) // 2, 1))
 
     def entry(kind, owner, me):
         if kind == 0:
             return st_ref.at[owner], stb.at[:, at(me, rows)]
-        if kind == 1:
-            return k_ref.at[:, at(owner, kcols)], kw.at[0, at(me, rows), :]
-        if kind == 2:
-            return v_ref.at[:, at(owner, kcols)], vw.at[0, at(me, rows), :]
-        g, which = (kind - 3) // 2, (kind - 3) % 2
+        if kind < first_wide:
+            g, which = (kind - 1) // 2, (kind - 1) % 2
+            from_cols = pl.ds(pl.multiple_of(owner * kcols + g * hd, hd), hd)
+            return (k_ref, v_ref)[which].at[:, from_cols], kv.at[0, g, which, at(me, rows), :]
+        g, which = (kind - first_wide) // 2, (kind - first_wide) % 2
         src, dst = ((q_ref, qb), (e_ref, eb))[which]
         from_cols = pl.ds(pl.multiple_of(owner * cols + g * gw, hd), gw)
         return src.at[:, from_cols], dst.at[at(me, rows), pl.ds(g * gw, gw)]
 
-    kinds = 3 + 2 * groups
+    first_wide = 1 + 2 * groups
+    kinds = 1 + 4 * groups
 
     def entry_copy(kind, r):
         peer = lax.rem(h + r, n)
@@ -84,7 +92,7 @@
         src, dst = entry(kind, h, h)
         return pltpu.make_async_copy(src, dst, loc_sem.at[kind])
 
-    for kind in (1, 2, 0) + tuple(range(3, kinds)):
+    for kind in tuple(range(1, first_wide)) + (0,) + tuple(range(first_wide, kinds)):
         entry_own(kind).start()
         for r in range(1, n):
             entry_copy(kind, r).start()
@@ -94,17 +102,76 @@
         for r in range(1, n):
             entry_copy(kind, r).wait_recv()
 
-    def forward(which, d):
-        buf = (kw, vw)[which]
+    def hand(g, step, slot, to_slot, to):
         return pltpu.make_async_remote_copy(
-            src_ref=buf.at[0], dst_ref=buf.at[d], send_sem=fw_s.at[which, d - 1], recv_sem=fw_r.at[which, d - 1],
-            device_id={"seq": s + d}, device_id_type=MESH)
-
-    def partial(which, g, d):
+            src_ref=kv.at[slot, g], dst_ref=kv.at[to_slot, g], send_sem=fw_s.at[g, step],
+            recv_sem=fw_r.at[g, to_slot - 1], device_id={"seq": to}, device_id_type=MESH)
+
+    def hand_steps(g):
+        return (
+            (has_up, hand(g, 0, 0, 2, s + 2)),
+            (even, hand(g, 1, 0, 1, side)),
+            (has_down & odd, hand(g, 2, 2, 1, side)),
+            (has_down & even, hand(g, 2, 2, 3, side)),
+            (has_down & even & has_up, hand(g, 3, 1, 3, s + 2)),
+        )
+
+    def hand_start(g, steps):
+        for i in steps:
+            cond, copy = hand_steps(g)[i]
+
+            @pl.when(cond)
+            def _():
+                copy.start()
+
+    def got(g, d):
+        @pl.when(s >= d)
+        def _():
+            hand(g, 0, 0, d, side).wait_recv()
+
+    def back(g, d, into, to):
         return pltpu.make_async_remote_copy(
-            src_ref=part_s.at[which, g, d - 1], dst_ref=part_r.at[which, g, d - 1],
-            send_sem=pt_s.at[which, g, d - 1], recv_sem=pt_r.at[which, g, d - 1],
-            device_id={"seq": s - d}, device_id_type=MESH)
+            src_ref=part_s.at[g, d - 1], dst_ref=part_r.at[g, into], send_sem=pt_s.at[g, d - 1],
+            recv_sem=pt_r.at[g, into], device_id={"seq": to}, device_id_type=MESH)
+
+    def join(g, into):
+        back(g, 1, into, side).wait_recv()
+        acck[...] += part_r[g, into, 0].astype(jnp.float32)
+        accv[...] += part_r[g, into, 1].astype(jnp.float32)
+
+    def put(g, d):
+        part_s[g, d - 1, 0] = acck[...].astype(jnp.bfloat16)
+        part_s[g, d - 1, 1] = accv[...].astype(jnp.bfloat16)
+
+    def pass_back(g, d):
+        if d == 3:
+            put(g, 3)
+
+            @pl.when(even)
+            def _():
+                back(g, 3, 0, s - 2).start()
+
+            @pl.when(odd)
+            def _():
+                back(g, 3, 1, side).start()
+        elif d == 1:
+            @pl.when(has_down & even & has_up)
+            def _():
+                join(g, 0)
+
+            put(g, 1)
+
+            @pl.when(even)
+            def _():
+                back(g, 1, 1, side).start()
+
+            @pl.when(odd)
+            def _():
+                back(g, 1, 3, side).start()
+        else:
+            join(g, 1)
+            put(g, 2)
+            back(g, 2, 2, s - 2).start()
 
     def leave(which, g, owner):
         src, dst, size, full = ((dqs, dq_out, gw, cols), (dks, dk_out, hd, kcols), (dvs, dv_out, hd, kcols))[which]
@@ -127,22 +194,26 @@
             leave_copy(which, g, r).start()
         leave_own(which, g).start()
 
-    for kind in (1, 2):
-        entry_wait(kind)
-    for d in range(1, REACH + 1):
-        @pl.when(s + d < seqs)
-        def _():
-            forward(0, d).start()
-            forward(1, d).start()
+    for g in range(groups):
+        entry_wait(1 + 2 * g)
+        entry_wait(2 + 2 * g)
+        hand_start(g, (0, 1))
     entry_wait(0)
+
+    def relay_two(g):
+        got(g, 2)
+        hand_start(g, (2, 3))
+
+    def relay_one(g):
+        got(g, 1)
+        hand_start(g, (4,))
 
     row_at = lax.broadcasted_iota(jnp.int32, (TILE, TILE), 0)
     col_at = lax.broadcasted_iota(jnp.int32, (TILE, TILE), 1)
 
     def tile(g, d, hf, qt):
         k_rows, q_rows = at(hf, TILE), at(qt, TILE)
-        kcol = pl.ds(g * hd, hd)
-        key, val = kw[d, k_rows, kcol], vw[d, k_rows, kcol]
+        key, val = kv[d, g, 0, k_rows, :], kv[d, g, 1, k_rows, :]
         key_t = key.T
         first = start_ref[0:1, q_rows] - (hf * TILE - d * block)
         allowed = row_at >= first
@@ -170,49 +241,48 @@
         acck[...] = jnp.zeros_like(acck)
         accv[...] = jnp.zeros_like(accv)
 
-        @pl.loop(0, halves)
-        def _(hf):
+        for hf in range(halves):
             low = hf if d == 0 else 0
             high = hf + 1 if d == REACH else halves
-
-            @pl.loop(low, high)
-            def _(qt):
+            for qt in range(low, high):
                 tile(g, d, hf, qt)
 
     def finish(g):
-        for d in range(1, REACH + 1):
-            @pl.when(s + d < seqs)
-            def _():
-                partial(0, g, d).wait_recv()
-                partial(1, g, d).wait_recv()
-                ownk[g] += part_r[0, g, d - 1].astype(jnp.float32)
-                ownv[g] += part_r[1, g, d - 1].astype(jnp.float32)
+        for cond, into in ((even, 3), (has_up, 2)):
+            @pl.when(cond)
+            def _():
+                back(g, 1, into, side).wait_recv()
+                ownk[g] += part_r[g, into, 0].astype(jnp.float32)
+                ownv[g] += part_r[g, into, 1].astype(jnp.float32)
+
         dks[:, g * hd : (g + 1) * hd] = (ownk[g] * scale).astype(jnp.bfloat16)
         dvs[:, g * hd : (g + 1) * hd] = ownv[g].astype(jnp.bfloat16)
         leave_start(1, g)
         leave_start(2, g)
 
+    relay_two(0)
     for g in range(groups):
-        entry_wait(3 + 2 * g)
-        entry_wait(4 + 2 * g)
+        if g == 0:
+            relay_two(1)
+            relay_one(0)
+        entry_wait(first_wide + 2 * g)
+        entry_wait(first_wide + 1 + 2 * g)
         dqt[...] = jnp.zeros_like(dqt)
-        order = range(REACH + 1) if g == 0 else range(REACH, -1, -1)
-        for step, d in enumerate(order):
+        for step, d in enumerate((0, 3, 1, 2) if g == 0 else (3, 1, 2, 0)):
             if d == 0:
                 compute(g, 0)
                 ownk[g] = acck[...]
                 ownv[g] = accv[...]
+                if g == 0:
+                    relay_one(1)
             else:
+                if d == 3:
+                    got(g, 3)
+
                 @pl.when(s >= d)
                 def _():
-                    if g == 0:
-                        forward(0, d).wait_recv()
-                        forward(1, d).wait_recv()
                     compute(g, d)
-                    part_s[0, g, d - 1] = acck[...].astype(jnp.bfloat16)
-                    part_s[1, g, d - 1] = accv[...].astype(jnp.bfloat16)
-                    partial(0, g, d).start()
-                    partial(1, g, d).start()
+                    pass_back(g, d)
             if g > 0 and step == 1:
                 finish(g - 1)
         for m in range(width):
@@ -229,17 +299,16 @@
     for kind in range(kinds):
         for r in range(1, n):
             entry_copy(kind, r).wait_send()
-    for d in range(1, REACH + 1):
-        @pl.when(s + d < seqs)
-        def _():
-            forward(0, d).wait_send()
-            forward(1, d).wait_send()
-
-        @pl.when(s >= d)
-        def _():
-            for g in range(groups):
-                partial(0, g, d).wait_send()
-                partial(1, g, d).wait_send()
+    for g in range(groups):
+        for cond, copy in hand_steps(g):
+            @pl.when(cond)
+            def _():
+                copy.wait_send()
+
+        for d in range(1, REACH + 1):
+            @pl.when(s >= d)
+            def _():
+                back(g, d, 0, side).wait_send()
 
 
 def shards(query, key, value, out, output_gradient, log_sum_exp, segment_ids):
@@ -260,7 +329,7 @@
     mine = lax.dynamic_slice_in_dim(segment_ids, base, block, 0)
     start = jnp.sum((segment_ids[:, None] < mine[None, :]).astype(jnp.int32), axis=0)[None, :] - base
     bf16, f32 = jnp.bfloat16, jnp.float32
-    kinds = 3 + 2 * groups
+    kinds = 1 + 4 * groups
     vmem = pl.BlockSpec(memory_space=pltpu.VMEM)
     dma = pltpu.SemaphoreType.DMA
     return pl.pallas_call(
@@ -276,25 +345,24 @@
             pltpu.VMEM((block, cols), bf16),
             pltpu.VMEM((block, cols), bf16),
             pltpu.VMEM((2 * heads, block), f32),
-            pltpu.VMEM((REACH + 1, block, kcols), bf16),
-            pltpu.VMEM((REACH + 1, block, kcols), bf16),
+            pltpu.VMEM((REACH + 1, groups, 2, block, hd), bf16),
             pltpu.VMEM((width, hd, block), f32),
             pltpu.VMEM((block, hd), f32),
             pltpu.VMEM((block, hd), f32),
             pltpu.VMEM((groups, block, hd), f32),
             pltpu.VMEM((groups, block, hd), f32),
-            pltpu.VMEM((2, groups, REACH, block, hd), bf16),
-            pltpu.VMEM((2, groups, REACH, block, hd), bf16),
+            pltpu.VMEM((groups, REACH, 2, block, hd), bf16),
+            pltpu.VMEM((groups, REACH + 1, 2, block, hd), bf16),
             pltpu.VMEM((block, cols), bf16),
             pltpu.VMEM((block, kcols), bf16),
             pltpu.VMEM((block, kcols), bf16),
             dma((kinds + 3 * groups,)),
             dma((kinds, n - 1)),
             dma((kinds, n - 1)),
-            dma((2, REACH)),
-            dma((2, REACH)),
-            dma((2, groups, REACH)),
-            dma((2, groups, REACH)),
+            dma((groups, REACH + 1)),
+            dma((groups, REACH)),
+            dma((groups, REACH)),
+            dma((groups, REACH + 1)),
             dma((3, groups, n - 1)),
             dma((3, groups, n - 1)),
         ],

time: 104 us -> 85.2 us (0.82)
  Pallas kernels: 94.6 us -> 75.2 us
    pallas_call x1, Pallas kernels: 94.6 us -> 75.2 us  [shards(): pl.pallas_call(functools.partial(kernel, n, seqs, groups, width), out_sha...]
where the time goes in v1:
time: 85.2 us; the launch traced here: 84.8 us
  Pallas kernels  75.2 us (88%)
  other arithmetic  4.59 us (5%)
  local copies, waits for them, and re-layouts  4.29 us (5%)
    pallas_call x1, Pallas kernels, shards(): pl.pallas_call(functools.partial(kernel, n, seqs, groups, width), out_sha...  75.2 us
    unnamed x12, local copies, waits for them, and re-layouts  4.16 us
    unnamed x1, other arithmetic  1.8 us

profile of v1, /device:TPU:15, one launch (start us, length us, event | category | flops | bytes accessed | tf_op | source)
XLA Modules:
  0.0 84.8 jit_solution(1954015998736570382)
XLA Ops:
  0.6 1.8 %multiply_bitcast_fusion = f32[16,8,32,128]{3,1,2,0:T(8,128)S(1)} fusion(bf16[128,4096]{1,0:T(8,128)(2,1)} %param.10, bf16[128,4096]{1,0:T(8,128)(2,1)} %e_ref.1), kind=kLoop, calls=%fused_computation.1 | loop fusion | flops 1572864 | bytes 4194304
  2.4 0.4 copy.12
  2.8 0.0 copy-start.2
  2.8 0.0 copy-start.3
  2.8 0.6 reduce_sum.18
  3.4 0.1 copy.11
  3.5 0.0 copy-done.2
  3.5 0.6 pad_maximum_fusion.st_ref
  4.2 0.0 copy-done.3
  4.2 0.1 dynamic_slice.3
  4.2 1.0 %convert_reduce_fusion = s32[512]{0:T(512)S(1)} fusion(s32[512]{0:T(512)S(1)} %dynamic_slice.3, s32[4096]{0:T(1024)S(1)} %copy-done.3), kind=kLoop, calls=%fused_computation | loop fusion | flops 6290944 | bytes 20480 | tf_op jit(solution)/shard_map/reduce_sum | solution.py:330
  5.2 0.6 broadcast_subtract_fusion
  5.8 75.2 %shard_map.94 = (bf16[128,4096]{1,0:T(8,128)(2,1)}, bf16[128,1024]{1,0:T(8,128)(2,1)}, bf16[128,1024]{1,0:T(8,128)(2,1)}) custom-call(bf16[128,4096]{1,0:T(8,128)(2,1)} %q_ref.1, bf16[128,4096]{1,0:T(8,128)(2,1)} %e_ref.1, bf16[128,1024]{1,0:T(8,128)(2,1)} %k_ref.1, bf16[128,1024]{1,0:T(8,128)(2,1)} %v_ref.1, f32[4,16,128]{2,1,0:T(8,128)} %pad_maximum_fusion.st_ref, ...), custom_call_target="tpu_custom_call" | custom-call | tf_op jit(solution)/shard_map/pallas_call | solution.py:335
  81.0 0.0 copy-start.1
  81.0 0.0 copy-start
  81.0 2.3 %copy.16 = bf16[128,4096]{1,0:T(8,128)(2,1)} copy(bf16[128,4096]{1,0:T(8,128)(2,1)} %get-tuple-element.6) | data formatting | bytes 2097152
  83.4 0.0 copy-done.1
  83.4 0.7 copy.17
  84.1 0.0 copy-done
  84.1 0.7 copy.18
  (1 shorter events, 0.0 us)
Async XLA Ops:
  2.8 0.7 copy-start.2
  2.8 1.3 %copy-start.3 = (s32[4096]{0:T(1024)S(1)}, s32[4096]{0:T(1024)}, u32[]{:S(2)}) copy-start(s32[4096]{0:T(1024)} %param.13) | copy-start | bytes 49156
  81.0 2.4 %copy-start.1 = (bf16[128,1024]{1,0:T(8,128)(2,1)S(1)}, bf16[128,1024]{1,0:T(8,128)(2,1)}, u32[]{:S(2)}) copy-start(bf16[128,1024]{1,0:T(8,128)(2,1)} %get-tuple-element.7) | copy-start | bytes 786436
  81.0 3.1 %copy-start = (bf16[128,1024]{1,0:T(8,128)(2,1)S(1)}, bf16[128,1024]{1,0:T(8,128)(2,1)}, u32[]{:S(2)}) copy-start(bf16[128,1024]{1,0:T(8,128)(2,1)} %get-tuple-element.8) | copy-start | bytes 786436

commit v2 on v1

--- a/solution.py
+++ b/solution.py
@@ -26,9 +26,9 @@
 
 def kernel(
     n, seqs, groups, width,
-    q_ref, e_ref, k_ref, v_ref, st_ref, start_ref,
+    q_ref, e_ref, k_ref, v_ref, o_ref, lse_ref, start_ref,
     dq_out, dk_out, dv_out,
-    qb, eb, stb, kv, dqt, acck, accv, ownk, ownv, part_s, part_r, dqs, dks, dvs,
+    st_ref, qb, eb, stb, kv, dqt, acck, accv, ownk, ownv, part_s, part_r, dqs, dks, dvs,
     loc_sem, in_s, in_r, fw_s, fw_r, pt_s, pt_r, out_s, out_r,
 ):
     s = lax.axis_index("seq")
@@ -92,10 +92,24 @@
         src, dst = entry(kind, h, h)
         return pltpu.make_async_copy(src, dst, loc_sem.at[kind])
 
-    for kind in tuple(range(1, first_wide)) + (0,) + tuple(range(first_wide, kinds)):
+    def entry_start(kind):
         entry_own(kind).start()
         for r in range(1, n):
             entry_copy(kind, r).start()
+
+    for kind in range(1, first_wide):
+        entry_start(kind)
+    lse_rows = (lse_ref[...] * LOG2E).T
+    for owner in range(n):
+        st_ref[owner, 0:heads, :] = lse_rows[owner * heads : (owner + 1) * heads, :]
+        for j in range(heads):
+            hcol = pl.ds((owner * heads + j) * hd, hd)
+            product = e_ref[:, hcol].astype(jnp.float32) * o_ref[:, hcol].astype(jnp.float32)
+            st_ref[owner, heads + j : heads + j + 1, :] = jnp.sum(product.T, axis=0, keepdims=True)
+    entry_start(first_wide)
+    entry_start(0)
+    for kind in range(first_wide + 1, kinds):
+        entry_start(kind)
 
     def entry_wait(kind):
         entry_own(kind).wait()
@@ -319,12 +333,6 @@
     cols, kcols = query.shape[1] // n, key.shape[1] // n
     groups, width = kcols // hd, cols // kcols
     heads = groups * width
-    delta = jnp.sum(
-        (output_gradient.astype(jnp.float32) * out.astype(jnp.float32)).reshape(rows, -1, hd), axis=2
-    )
-    stats = jnp.concatenate(
-        [(log_sum_exp * LOG2E).T.reshape(n, heads, rows), delta.T.reshape(n, heads, rows)], axis=1
-    )
     base = lax.axis_index("seq") * block
     mine = lax.dynamic_slice_in_dim(segment_ids, base, block, 0)
     start = jnp.sum((segment_ids[:, None] < mine[None, :]).astype(jnp.int32), axis=0)[None, :] - base
@@ -339,9 +347,10 @@
             jax.ShapeDtypeStruct(key.shape, bf16),
             jax.ShapeDtypeStruct(value.shape, bf16),
         ],
-        in_specs=[vmem] * 6,
+        in_specs=[vmem] * 7,
         out_specs=[vmem] * 3,
         scratch_shapes=[
+            pltpu.VMEM((n, 2 * heads, rows), f32),
             pltpu.VMEM((block, cols), bf16),
             pltpu.VMEM((block, cols), bf16),
             pltpu.VMEM((2 * heads, block), f32),
@@ -367,7 +376,7 @@
             dma((3, groups, n - 1)),
         ],
         compiler_params=pltpu.CompilerParams(collective_id=0, has_side_effects=True),
-    )(query, output_gradient, key, value, stats, start)
+    )(query, output_gradient, key, value, out, log_sum_exp, start)
 
 
 def solution(mesh):

time: 85.2 us -> 86.9 us (1.020)
  other arithmetic: 4.59 us -> 2.25 us
  Pallas kernels: 75.2 us -> 77.5 us
  local copies, waits for them, and re-layouts: 4.29 us -> 5.97 us
    pallas_call x1, Pallas kernels: 75.2 us -> 77.5 us  [shards(): pl.pallas_call(functools.partial(kernel, n, seqs, groups, width), out_sha...]
    unnamed x1 -> x0, other arithmetic: 1.8 us -> none
    unnamed x12 -> x8, local copies, waits for them, and re-layouts: 4.16 us -> 5.2 us
where the time goes in v2:
time: 86.9 us; the launch traced here: 86.4 us
  Pallas kernels  77.5 us (89%)
  local copies, waits for them, and re-layouts  5.97 us (7%)
  other arithmetic  2.25 us (3%)
    pallas_call x1, Pallas kernels, shards(): pl.pallas_call(functools.partial(kernel, n, seqs, groups, width), out_sha...  77.5 us
    unnamed x8, local copies, waits for them, and re-layouts  5.2 us

profile of v2, /device:TPU:15, one launch (start us, length us, event | category | flops | bytes accessed | tf_op | source)
XLA Modules:
  0.0 86.4 jit_solution(5369424374864825351)
XLA Ops:
  0.6 0.8 dynamic_slice.3
  1.4 1.7 %convert_reduce_fusion = s32[512]{0:T(512)S(1)} fusion(s32[512]{0:T(512)S(1)} %dynamic_slice.3, s32[4096]{0:T(1024)} %param.13), kind=kLoop, calls=%fused_computation | loop fusion | flops 6290944 | bytes 20480 | tf_op jit(solution)/shard_map/reduce_sum | solution.py:338
  3.1 0.6 broadcast_subtract_fusion
  3.7 1.4 %copy.11.lse_ref = f32[128,32]{1,0:T(8,128)} copy(f32[128,32]{0,1:T(8,128)} %param.12) | data formatting | bytes 32768 | tf_op args[5]
  5.1 77.5 %shard_map.94 = (bf16[128,4096]{1,0:T(8,128)(2,1)}, bf16[128,1024]{1,0:T(8,128)(2,1)}, bf16[128,1024]{1,0:T(8,128)(2,1)}) custom-call(bf16[128,4096]{1,0:T(8,128)(2,1)} %q_ref.1, bf16[128,4096]{1,0:T(8,128)(2,1)} %e_ref.1, bf16[128,1024]{1,0:T(8,128)(2,1)} %k_ref.1, bf16[128,1024]{1,0:T(8,128)(2,1)} %v_ref.1, bf16[128,4096]{1,0:T(8,128)(2,1)} %o_ref.1, ...), custom_call_target="tpu_custom_call" | custom-call | tf_op jit(solution)/shard_map/pallas_call | solution.py:343
  82.6 0.0 copy-start.1
  82.6 0.0 copy-start
  82.6 2.3 %copy.15 = bf16[128,4096]{1,0:T(8,128)(2,1)} copy(bf16[128,4096]{1,0:T(8,128)(2,1)} %get-tuple-element.6) | data formatting | bytes 2097152
  85.0 0.0 copy-done.1
  85.0 0.7 copy.16
  85.7 0.0 copy-done
  85.7 0.7 copy.17
Async XLA Ops:
  82.6 2.4 %copy-start.1 = (bf16[128,1024]{1,0:T(8,128)(2,1)S(1)}, bf16[128,1024]{1,0:T(8,128)(2,1)}, u32[]{:S(2)}) copy-start(bf16[128,1024]{1,0:T(8,128)(2,1)} %get-tuple-element.7) | copy-start | bytes 786436
  82.6 3.1 %copy-start = (bf16[128,1024]{1,0:T(8,128)(2,1)S(1)}, bf16[128,1024]{1,0:T(8,128)(2,1)}, u32[]{:S(2)}) copy-start(bf16[128,1024]{1,0:T(8,128)(2,1)} %get-tuple-element.8) | copy-start | bytes 786436
